TPU v7x, 32 devices: a whole 2x2x4 slice. The times are simulated.
32 devices in a mesh: mom: 4 (over y, core), tm: 4 (over z), pt: 2 (over x).
Axes of the slice: x: 2, y: 2, z: 4, core: 2. Of those that a mesh axis runs over, the one named last changes fastest.
Arguments:
- chi_time: bfloat16 [16, 8, 896, 896], P('tm', 'mom', 'pt'), may hold values from -4 to 4
- green: bfloat16 [8, 16, 896, 896], P('mom', 'tm', 'pt'), may hold values from -6 to 6
- band_coeffs: bfloat16 [896, 1024], replicated, may hold values from -1 to 1
Outputs:
- self_energy: float32 [8, 16, 1024], P('mom', 'tm', 'pt')
All inputs are finite; a program needn't handle non-finite values.
Results may differ from a plain program's by a relative error of at most 0.009.
Values may be sent and summed in bfloat16 or wider, within the bound.
A program may use at most 128 MiB of HBM per device.

v0:
```python
import math

import jax
import jax.numpy as jnp
from jax import lax
from jax.sharding import PartitionSpec as P

ORDER = 8


COUPLING = 0.8


def cosine_table(count):
    index = jnp.arange(count, dtype=jnp.float32) + 0.5
    angle = jnp.pi * index[:, None] * index[None, :] / count
    return (jnp.sqrt(jnp.float32(2.0 / count)) * jnp.cos(angle)).astype(jnp.bfloat16)


def hartley_table(count):
    index = jnp.arange(count, dtype=jnp.float32)
    angle = 2.0 * jnp.pi * index[:, None] * index[None, :] / count
    return (jnp.cos(angle) + jnp.sin(angle)) / jnp.sqrt(jnp.float32(count))


def series(tiles, operand):
    power = tiles
    total = tiles.astype(jnp.float32)
    for term in range(ORDER - 1):
        power = jnp.einsum(
            "arq,aqs->ars", power, operand, preferred_element_type=jnp.float32
        ).astype(jnp.bfloat16)
        total = total + power.astype(jnp.float32)
    return total.astype(jnp.bfloat16)


def local(chi_time, green, band_coeffs):
    times_dev, moms_dev, rows_dev, points = chi_time.shape
    count_t = times_dev * lax.axis_size("tm")
    count_k = moms_dev * lax.axis_size("mom")
    cosine = cosine_table(count_t)
    hartley = hartley_table(count_k)
    scale = COUPLING / math.sqrt(points)
    regrouped = lax.all_to_all(chi_time, "tm", split_axis=2, concat_axis=0, tiled=True)
    mixed = jnp.einsum("wt,tkpq->wkpq", cosine, regrouped, preferred_element_type=jnp.float32)
    mixed = (scale * mixed).astype(jnp.bfloat16)
    freq = lax.all_to_all(mixed, "tm", split_axis=0, concat_axis=2, tiled=True)
    tiles = freq.reshape(times_dev * moms_dev, rows_dev, points)
    whole_tiles = lax.all_gather(tiles, "pt", axis=1, tiled=True)
    screened = series(tiles, whole_tiles)
    screened = screened.reshape(times_dev, moms_dev, rows_dev, points)
    spread = lax.all_to_all(
        lax.all_to_all(screened, "mom", split_axis=2, concat_axis=1, tiled=True),
        "tm",
        split_axis=3,
        concat_axis=0,
        tiled=True,
    )
    timed = jnp.einsum("tw,wkpq->tkpq", cosine, spread, preferred_element_type=jnp.float32)
    cells = jnp.einsum("rk,tkpq->rtpq", hartley, timed, precision=lax.Precision.HIGHEST)
    lattice = lax.all_to_all(
        lax.all_to_all(cells, "mom", split_axis=0, concat_axis=2, tiled=True),
        "tm",
        split_axis=1,
        concat_axis=3,
        tiled=True,
    )
    sigma = (green.astype(jnp.float32) * lattice).astype(jnp.bfloat16)
    own_coeffs = lax.dynamic_slice_in_dim(band_coeffs, lax.axis_index("pt") * rows_dev, rows_dev, 0)
    applied = jnp.einsum("rtpq,qn->rtpn", sigma, band_coeffs, preferred_element_type=jnp.float32)
    partial_sums = jnp.sum(applied * own_coeffs.astype(jnp.float32)[None, None], axis=2)
    return lax.psum_scatter(partial_sums, "pt", scatter_dimension=2, tiled=True)


def solution(mesh):
    placed = (P("tm", "mom", "pt", None), P("mom", "tm", "pt", None), P())
    return jax.shard_map(
        local, mesh=mesh, in_specs=placed, out_specs=P("mom", "tm", "pt"), check_vma=False
    )
```

profile of v0, /device:TPU:0, one launch (start us, length us, event | category | flops | bytes accessed | tf_op | source)
XLA Modules:
  0.0 1541.4 jit_solution(9406410548873897525)
XLA Ops:
  6.5 10.4 copy.49
  17.0 6.3 all-to-all-start
  23.3 0.0 all-gather.2.cloned.1.call-start
  23.3 141.6 %all-to-all-done = bf16[4,2,448,896]{3,0,1,2:T(4,128)(2,1)} async-done(((bf16[4,2,448,896]{3,0,1,2:T(4,128)(2,1)}), bf16[4,2,448,896]{3,0,1,2:T(4,128)(2,1)}, u32[]{:S(2)}, u32[]{:S(2)}) %all-to-all-start) | async-done | bytes 6422560 | tf_op jit(solution)/shard_map/all_to_all | solution.py:44
  164.9 7.7 copy.78
  172.6 11.0 all_to_all.79
  183.6 4.7 multiply_convert_fusion.1
  188.3 1.3 copy.51
  189.6 143.4 %all_to_all.105 = bf16[16,2,112,896]{3,2,1,0:T(8,128)(2,1)S(1)} all-to-all(bf16[16,2,112,896]{3,2,1,0:T(8,128)(2,1)S(1)} %copy.51), channel_id=1, replica_groups=mesh['mom'=4,'tm'=4,'pt'=2] {'tm'}, dimensions={0} | all-to-all | bytes 12845056 | tf_op jit(solution)/shard_map/all_to_all | solution.py:47
  333.1 3.3 copy.52
  336.3 0.0 all-gather.2.cloned.1.call-update
  336.4 154.2 %all-gather.2.cloned.1.call-done = bf16[8,896,896]{2,1,0:T(8,128)(2,1)} async-done(((bf16[8,448,896]{2,1,0:T(8,128)(2,1)}), bf16[8,896,896]{2,1,0:T(8,128)(2,1)}) %all-gather.2.cloned.1.call-update) | async-done | bytes 12845072 | tf_op jit(solution)/shard_map/all_gather | solution.py:49
  490.6 0.0 copy-start
  490.6 15.7 %convolution_convert_fusion.6 = bf16[8,448,896]{2,1,0:T(8,128)(2,1)} fusion(bf16[8,448,896]{2,1,0:T(8,128)(2,1)} %bitcast.63, bf16[8,896,896]{2,1,0:T(8,128)(2,1)} %all-gather.2.cloned.1.call-done), kind=kOutput, calls=%fused_computation.14 | convolution fusion | flops 5757796352 | bytes 25690112 | tf_op jit(solution)/shard_map/arq,aqs->ars/dot_general | solution.py:30
  506.2 0.0 copy-done
  506.2 12.5 convolution_convert_fusion.5
  518.7 12.5 convolution_convert_fusion.4
  531.2 12.6 convolution_convert_fusion.3
  543.9 12.4 convolution_convert_fusion.2
  556.3 12.4 convolution_convert_fusion.1
  568.7 25.5 %add_convert_fusion = bf16[8,448,896]{2,1,0:T(8,128)(2,1)} fusion(bf16[8,448,896]{2,1,0:T(8,128)(2,1)} %convolution_convert_fusion.1, bf16[8,448,896]{2,1,0:T(8,128)(2,1)} %convolution_convert_fusion.2, bf16[8,448,896]{2,1,0:T(8,128)(2,1)} %convolution_convert_fusion.3, bf16[8,448,896]{2,1,0:T(8,128)(2,1)} %convolution_convert_fusion.4, ...), kind=kOutput, calls=%fused_computation.4 | convolution fusion | flops 5809176576 | bytes 64225280 | tf_op jit(solution)/shard_map/arq,aqs->ars/dot_general | solution.py:30
  594.2 28.6 %copy.53 = bf16[4,2,448,896]{3,1,0,2:T(2,128)(2,1)S(1)} copy(bf16[4,2,448,896]{3,2,1,0:T(8,128)(2,1)} %bitcast.69) | data formatting | bytes 12845056 | tf_op jit(solution)/shard_map/reshape | solution.py:51
  622.8 74.7 %all_to_all.106 = bf16[4,2,448,896]{3,1,0,2:T(2,128)(2,1)S(1)} all-to-all(bf16[4,2,448,896]{3,1,0,2:T(2,128)(2,1)S(1)} %copy.53), channel_id=1, replica_groups=mesh['mom'=4,'tm'=4,'pt'=2] {'mom'}, dimensions={2} | all-to-all | bytes 12845056 | tf_op jit(solution)/shard_map/all_to_all | solution.py:53
  697.5 1.1 copy.54
  698.6 3.3 copy.55
  701.9 11.8 copy.56
  713.7 5.4 all-to-all-start.3
  719.2 160.5 %all-to-all-done.3 = bf16[4,8,112,896]{2,1,0,3:T(8,128)(2,1)} async-done(((bf16[4,8,112,896]{2,1,0,3:T(8,128)(2,1)}), bf16[4,8,112,896]{2,1,0,3:T(8,128)(2,1)}, u32[]{:S(2)}, u32[]{:S(2)}) %all-to-all-start.3) | async-done | bytes 6422560 | tf_op jit(solution)/shard_map/all_to_all | solution.py:52
  879.7 11.2 copy.69
  890.9 7.3 copy.58
  898.1 7.6 fusion.2
  905.8 29.7 %fusion = f32[8,16,112,224]{3,0,2,1:T(8,128)} fusion(f32[16,8,112,224]{3,0,2,1:T(8,128)S(1)} %fusion.2, f32[8]{0:T(128)S(1)} %iota_multiply_fusion), kind=kOutput, calls=%fused_computation | convolution fusion | flops 308281600 | bytes 25690144 | tf_op jit(solution)/shard_map/rk,tkpq->rtpq/dot_general | solution.py:60
  935.5 15.1 copy.61
  950.5 170.7 %all_to_all.107 = f32[8,16,112,224]{3,2,1,0:T(8,128)} all-to-all(f32[8,16,112,224]{3,2,1,0:T(8,128)} %copy.61), channel_id=1, replica_groups=mesh['mom'=4,'tm'=4,'pt'=2] {'mom'}, dimensions={0} | all-to-all | bytes 25690112 | tf_op jit(solution)/shard_map/all_to_all | solution.py:62
  1121.3 11.8 copy.62
  1133.1 11.9 copy.63
  1144.9 6.6 all-to-all-start.5
  1151.6 0.0 reduce-scatter.4.cloned.1.call-start
  1151.6 1.4 dynamic-slice_convert_fusion
  1153.0 316.4 %all-to-all-done.5 = f32[2,16,448,224]{3,2,0,1:T(8,128)} async-done(((f32[2,16,448,224]{3,2,0,1:T(8,128)}), f32[2,16,448,224]{3,2,0,1:T(8,128)}, u32[]{:S(2)}, u32[]{:S(2)}) %all-to-all-start.5) | async-done | bytes 12845088 | tf_op jit(solution)/shard_map/all_to_all | solution.py:61
  1469.4 18.9 %copy.65 = f32[2,4,448,4,224]{4,3,2,1,0:T(4,128)} copy(f32[2,4,448,4,224]{4,2,0,1,3:T(8,128)} %bitcast.23) | data formatting | bytes 25690112 | tf_op jit(solution)/shard_map/all_to_all | solution.py:61
  1488.4 17.1 %all_to_all.98 = f32[2,4,448,896]{3,2,1,0:T(8,128)} reshape(f32[2,4,448,4,224]{4,3,2,1,0:T(4,128)} %copy.65) | data formatting | bytes 25690112 | tf_op jit(solution)/shard_map/all_to_all | solution.py:61
  1505.5 12.3 multiply_reduce_fusion
  1517.8 0.6 copy.71
  1518.4 1.4 reshape.28
  1519.8 0.0 reduce-scatter.4.cloned.1.call-update
  1519.8 12.3 reduce-scatter.4.cloned.1.call-done
  1532.0 1.3 reshape.29
  1533.3 0.8 copy.72
  (2 shorter events, 0.0 us)
Async XLA Ops:
  17.0 147.9 %all-to-all-start = ((bf16[4,2,448,896]{3,0,1,2:T(4,128)(2,1)}), bf16[4,2,448,896]{3,0,1,2:T(4,128)(2,1)}, u32[]{:S(2)}, u32[]{:S(2)}) async-start(bf16[4,2,448,896]{3,0,1,2:T(4,128)(2,1)} %copy.49), calls=%async_computation | async-start | bytes 12845056 | tf_op jit(solution)/shard_map/all_to_all | solution.py:44
  23.3 467.2 %all-gather.2.cloned.1.call-start = ((), (), s32[]{:S(2)}) async-start(), calls=%async_computation.7 | async-start | bytes 19267584 | tf_op jit(solution)/shard_map/all_gather | solution.py:49
  490.6 15.7 %copy-start = (bf16[8,896,896]{2,1,0:T(8,128)(2,1)S(1)}, bf16[8,896,896]{2,1,0:T(8,128)(2,1)}, u32[]{:S(2)}) copy-start(bf16[8,896,896]{2,1,0:T(8,128)(2,1)} %all-gather.2.cloned.1.call-done) | copy-start | bytes 38535172
  713.7 166.0 %all-to-all-start.3 = ((bf16[4,8,112,896]{2,1,0,3:T(8,128)(2,1)}), bf16[4,8,112,896]{2,1,0,3:T(8,128)(2,1)}, u32[]{:S(2)}, u32[]{:S(2)}) async-start(bf16[4,8,112,896]{2,1,0,3:T(8,128)(2,1)} %copy.56), calls=%async_computation.3 | async-start | bytes 14680064 | tf_op jit(solution)/shard_map/all_to_all | solution.py:52
  1144.9 324.5 %all-to-all-start.5 = ((f32[2,16,448,224]{3,2,0,1:T(8,128)}), f32[2,16,448,224]{3,2,0,1:T(8,128)}, u32[]{:S(2)}, u32[]{:S(2)}) async-start(f32[2,16,448,224]{3,2,0,1:T(8,128)} %copy.63), calls=%async_computation.5 | async-start | bytes 29360128 | tf_op jit(solution)/shard_map/all_to_all | solution.py:61
  1151.6 380.4 %reduce-scatter.4.cloned.1.call-start = ((), (), s32[]{:S(2)}) async-start(), calls=%async_computation.8 | async-start | bytes 786432
Sparse Core Ops, SparseCore 0:
  336.5 154.0 all-gather.1
  1519.9 12.0 reduce-scatter.3
where the time goes:
time: 1550 us; the launch traced here: 1540 us
  waiting for transfers between devices  785 us (51%)
  blocking collectives  389 us (25%)
  local copies, waits for them, and re-layouts  176 us (11%)
  matrix products  158 us (10%)
  starting transfers between devices  18.5 us (1%)
    all_to_all x1, waiting for transfers between devices, local(): lax.all_to_all(lax.all_to_all(cells, 'mom', split_axis=0, concat_axis=2,...  316 us
    all_to_all x1, blocking collectives, local(): lax.all_to_all(cells, 'mom', split_axis=0, concat_axis=2, tiled=True)  171 us
    all_to_all x1, waiting for transfers between devices, local(): lax.all_to_all(lax.all_to_all(screened, 'mom', split_axis=2, concat_axis=...  161 us
    all_gather x1, waiting for transfers between devices, local(): whole_tiles = lax.all_gather(tiles, 'pt', axis=1, tiled=True)  154 us
    all_to_all x1, blocking collectives, local(): freq = lax.all_to_all(mixed, 'tm', split_axis=0, concat_axis=2, tiled=True)  143 us
    all_to_all x1, waiting for transfers between devices, local(): lax.all_to_all(chi_time, 'tm', split_axis=2, concat_axis=0, tiled=True)  142 us
    dot_general x7, matrix products, series(): jnp.einsum('arq,aqs->ars', power, operand, preferred_element_type=jnp.flo...  104 us
    all_to_all x1, blocking collectives, local(): lax.all_to_all(screened, 'mom', split_axis=2, concat_axis=1, tiled=True)  74.7 us
  transfers between devices with their start and end apart: 5, of which 5 were waited for; matrix products, arithmetic and copies ran while one was open for 0% of the time, Pallas kernels for 0%

commit v1 on v0

v1 whole, which is shorter than its diff:
```python
import math

import jax
import jax.numpy as jnp
from jax import lax
from jax.sharding import Mesh, PartitionSpec as P

COUPLING = 0.8
JOINT = True


def cosine_table(count):
    index = jnp.arange(count, dtype=jnp.float32) + 0.5
    angle = jnp.pi * index[:, None] * index[None, :] / count
    return (jnp.sqrt(jnp.float32(2.0 / count)) * jnp.cos(angle)).astype(jnp.bfloat16)


def hartley_table(count):
    index = jnp.arange(count, dtype=jnp.float32)
    angle = 2.0 * jnp.pi * index[:, None] * index[None, :] / count
    return (jnp.cos(angle) + jnp.sin(angle)) / jnp.sqrt(jnp.float32(count))


def product(left, right):
    return jnp.einsum("apq,aqs->aps", left, right, preferred_element_type=jnp.float32)


def series(tiles):
    square = product(tiles, tiles).astype(jnp.bfloat16)
    two = (tiles.astype(jnp.float32) + square.astype(jnp.float32)).astype(jnp.bfloat16)
    fourth = product(square, square).astype(jnp.bfloat16)
    four = (two.astype(jnp.float32) + product(two, square)).astype(jnp.bfloat16)
    return (four.astype(jnp.float32) + product(four, fourth)).astype(jnp.bfloat16)


def local(chi_time, green, band_coeffs):
    times_dev, moms_dev, rows_dev, points = chi_time.shape
    momenta, high, low = lax.axis_size("mom"), lax.axis_size("th"), lax.axis_size("tl")
    count_t = times_dev * high * low
    count_k = moms_dev * momenta
    part = rows_dev // low
    piece = part // momenta
    own_k = moms_dev // high
    cosine = cosine_table(count_t)
    hartley = hartley_table(count_k).astype(jnp.bfloat16)
    scale = COUPLING / math.sqrt(points)

    cells_dev = green.shape[0]
    spread = green.reshape(cells_dev, times_dev, low, momenta, piece, points)
    spread = spread.transpose(3, 0, 1, 2, 4, 5)
    spread = lax.all_to_all(spread, "mom", split_axis=0, concat_axis=0, tiled=True)
    spread = spread.reshape(count_k, times_dev, low, piece, points)

    blocks = chi_time.reshape(times_dev, high, own_k, low, part, points)
    blocks = blocks.transpose(1, 3, 0, 2, 4, 5).reshape(high * low, times_dev * own_k, part, points)
    blocks = lax.all_to_all(blocks, ("th", "tl"), split_axis=0, concat_axis=0, tiled=True)
    blocks = blocks.reshape(count_t, own_k, part, points)
    mixed = jnp.einsum("wt,tkpq->wkpq", cosine, blocks, preferred_element_type=jnp.float32)
    mixed = (scale * mixed).astype(jnp.bfloat16).reshape(count_t * own_k, part, points)
    tiles = lax.all_to_all(mixed, ("pt", "tl"), split_axis=0, concat_axis=1, tiled=True)
    screened = series(tiles)
    back = lax.all_to_all(screened, ("pt", "tl"), split_axis=1, concat_axis=0, tiled=True)
    back = back.reshape(count_t, own_k, part, points)
    timed = jnp.einsum("tw,wkpq->tkpq", cosine, back, preferred_element_type=jnp.float32)
    timed = timed.astype(jnp.bfloat16)

    if JOINT:
        timed = timed.reshape(high * low, times_dev, own_k, momenta, piece, points)
        timed = timed.transpose(3, 0, 1, 2, 4, 5)
        timed = timed.reshape(momenta * high * low, times_dev, own_k, piece, points)
        timed = lax.all_to_all(timed, ("mom", "th", "tl"), split_axis=0, concat_axis=0, tiled=True)
    else:
        timed = timed.reshape(high * low, times_dev, own_k, part, points)
        timed = lax.all_to_all(timed, ("th", "tl"), split_axis=0, concat_axis=0, tiled=True)
        timed = timed.reshape(high * low, times_dev, own_k, momenta, piece, points)
        timed = timed.transpose(3, 0, 1, 2, 4, 5)
        timed = lax.all_to_all(timed, "mom", split_axis=0, concat_axis=0, tiled=True)
    timed = timed.reshape(momenta, high, low, times_dev, own_k, piece, points)
    timed = timed.transpose(0, 1, 4, 3, 2, 5, 6).reshape(count_k, times_dev, low, piece, points)
    lattice = jnp.einsum("rk,ktlpq->rtlpq", hartley, timed, preferred_element_type=jnp.float32)
    sigma = (spread.astype(jnp.float32) * lattice).astype(jnp.bfloat16)

    own = lax.dynamic_slice_in_dim(band_coeffs, lax.axis_index("pt") * rows_dev, rows_dev, 0)
    own = own.reshape(low, momenta, piece, -1)
    own = lax.dynamic_index_in_dim(own, lax.axis_index("mom"), 1, keepdims=False)
    applied = jnp.einsum("rtlpq,qn->rtlpn", sigma, band_coeffs, preferred_element_type=jnp.float32)
    partial_sums = jnp.sum(applied * own.astype(jnp.float32)[None, None], axis=(2, 3))
    partial_sums = lax.psum_scatter(partial_sums, "mom", scatter_dimension=0, tiled=True)
    return lax.psum_scatter(partial_sums, "pt", scatter_dimension=2, tiled=True)


def solution(mesh):
    sizes = dict(mesh.shape)
    names, extents = [], []
    for name in mesh.axis_names:
        if name == "tm":
            names += ["th", "tl"]
            extents += [2, sizes[name] // 2]
        else:
            names.append(name)
            extents.append(sizes[name])
    fine = Mesh(mesh.devices.reshape(extents), tuple(names))
    tm = ("th", "tl")
    placed = (P(tm, "mom", "pt", None), P("mom", tm, "pt", None), P())
    return jax.shard_map(
        local, mesh=fine, in_specs=placed, out_specs=P("mom", tm, "pt"), check_vma=False
    )
```

time: 1550 us -> 749 us (0.48)
  waiting for transfers between devices: 785 us -> 410 us
  blocking collectives: 389 us -> 74.2 us
  matrix products: 158 us -> 91.6 us
  local copies, waits for them, and re-layouts: 176 us -> 118 us
    all_to_all x3 -> x1, blocking collectives: 389 us -> 74.2 us  [local(): lax.all_to_all(mixed, ('pt', 'tl'), split_axis=0, concat_axis=1, tiled=True)]
    all_to_all x3 -> x4, waiting for transfers between devices: 618 us -> 366 us  [the longest x1 142 us: local(): lax.all_to_all(blocks, ('th', 'tl'), split_axis=0, concat_axis=0, tiled=T...]
    all_gather x1 -> x0, waiting for transfers between devices: 154 us -> none  [local(): whole_tiles = lax.all_gather(tiles, 'pt', axis=1, tiled=True)]
    all_to_all x12 -> x3, local copies, waits for them, and re-layouts: 116 us -> 16.1 us  [the longest x1 7.73 us: local(): lax.all_to_all(screened, ('pt', 'tl'), split_axis=1, concat_axis=0, tiled...]
    dot_general x11 -> x7, matrix products: 158 us -> 91.6 us  [the longest x3 50.8 us: product(): jnp.einsum('apq,aqs->aps', left, right, preferred_element_type=jnp.float32)]
    reshape x1 -> x6, local copies, waits for them, and re-layouts: 28.6 us -> 64.9 us  [the longest x2 18.4 us: local(): timed = timed.reshape(high * low, times_dev, own_k, momenta, piece, points)]
    unnamed x3 -> x4, waiting for transfers between devices: 12.3 us -> 44.1 us
  transfers between devices with their start and end apart: 5 -> 6, of which waited for: 5 -> 6; matrix products, arithmetic and copies ran while one was open for 0% -> 8% of each run, Pallas kernels for 0% -> 0%
where the time goes in v1:
time: 749 us; the launch traced here: 739 us
  waiting for transfers between devices  410 us (55%)
  local copies, waits for them, and re-layouts  118 us (16%)
  matrix products  91.6 us (12%)
  blocking collectives  74.2 us (10%)
  starting transfers between devices  21.9 us (3%)
  between operations  14.4 us (2%)
  other arithmetic  8.66 us (1%)
    all_to_all x1, waiting for transfers between devices, local(): lax.all_to_all(blocks, ('th', 'tl'), split_axis=0, concat_axis=0, tiled=T...  142 us
    all_to_all x1, waiting for transfers between devices, local(): lax.all_to_all(timed, ('mom', 'th', 'tl'), split_axis=0, concat_axis=0, t...  133 us
    all_to_all x1, blocking collectives, local(): lax.all_to_all(mixed, ('pt', 'tl'), split_axis=0, concat_axis=1, tiled=True)  74.2 us
    all_to_all x1, waiting for transfers between devices, local(): lax.all_to_all(screened, ('pt', 'tl'), split_axis=1, concat_axis=0, tiled...  63.6 us
    dot_general x3, matrix products, product(): jnp.einsum('apq,aqs->aps', left, right, preferred_element_type=jnp.float32)  50.8 us
    unnamed x4, waiting for transfers between devices  44.1 us
    all_to_all x1, waiting for transfers between devices, local(): lax.all_to_all(spread, 'mom', split_axis=0, concat_axis=0, tiled=True)  27.5 us
    reshape x2, local copies, waits for them, and re-layouts, local(): timed = timed.reshape(high * low, times_dev, own_k, momenta, piece, points)  18.4 us
  transfers between devices with their start and end apart: 6, of which 6 were waited for; matrix products, arithmetic and copies ran while one was open for 8% of the time, Pallas kernels for 0%

profile of v1, /device:TPU:0, one launch (start us, length us, event | category | flops | bytes accessed | tf_op | source)
XLA Modules:
  0.0 738.9 jit_solution(15087316992124508674)
XLA Ops:
  6.5 0.0 copy-start
  6.5 10.6 %copy.26 = bf16[4,2,1,2,224,896]{5,0,4,3,1,2:T(4,128)(2,1)} copy(bf16[4,2,1,2,224,896]{5,4,3,1,0,2:T(8,128)(2,1)} %bitcast.70) | data formatting | bytes 12845056 | tf_op jit(solution)/shard_map/reshape | solution.py:54
  17.1 6.3 all-to-all-start.1
  23.5 141.6 %all-to-all-done.1 = bf16[4,4,224,896]{3,1,2,0:T(4,128)(2,1)} async-done(((bf16[4,4,224,896]{3,1,2,0:T(4,128)(2,1)}), bf16[4,4,224,896]{3,1,2,0:T(4,128)(2,1)}, u32[]{:S(2)}, u32[]{:S(2)}) %all-to-all-start.1) | async-done | bytes 6422560 | tf_op jit(solution)/shard_map/all_to_all | solution.py:56
  165.0 7.7 %copy.27 = bf16[4,4,224,896]{3,1,0,2:T(4,128)(2,1)} copy(bf16[4,4,224,896]{3,1,2,0:T(4,128)(2,1)} %all-to-all-done.1) | data formatting | bytes 12845056 | tf_op jit(solution)/shard_map/all_to_all | solution.py:56
  172.7 11.0 %reshape.71 = bf16[16,224,896]{2,0,1:T(8,128)(2,1)} reshape(bf16[4,4,224,896]{3,1,0,2:T(4,128)(2,1)} %copy.27) | data formatting | bytes 12845056 | tf_op jit(solution)/shard_map/reshape
  183.7 4.7 multiply_convert_fusion
  188.4 1.3 copy.28
  189.8 74.2 %all_to_all.48 = bf16[16,224,896]{2,1,0:T(8,128)(2,1)S(1)} all-to-all(bf16[16,224,896]{2,1,0:T(8,128)(2,1)S(1)} %copy.28), channel_id=1, replica_groups=mesh['mom'=4,'th'=2,'tl'=2,'pt'=2] {'pt','tl'}, dimensions={0} | all-to-all | bytes 12845056 | tf_op jit(solution)/shard_map/all_to_all | solution.py:60
  264.0 0.7 copy.29
  264.7 0.0 copy-start.1
  264.7 2.6 copy-done.1
  267.3 9.6 %convolution_convert_fusion.1 = bf16[4,896,896]{2,1,0:T(8,128)(2,1)} fusion(bf16[4,896,896]{2,1,0:T(8,128)(2,1)S(1)} %bitcast.72), kind=kOutput, calls=%fused_computation.13 | convolution fusion | flops 5757796352 | bytes 12845056 | tf_op jit(solution)/shard_map/apq,aqs->aps/dot_general | solution.py:25
  277.0 16.0 %add_convert_fusion.1 = bf16[4,896,896]{2,1,0:T(8,128)(2,1)} fusion(bf16[4,896,896]{2,1,0:T(8,128)(2,1)} %convolution_convert_fusion.1, bf16[4,896,896]{2,1,0:T(8,128)(2,1)} %bitcast.73), kind=kOutput, calls=%fused_computation.4 | convolution fusion | flops 5789908992 | bytes 19267584 | tf_op jit(solution)/shard_map/apq,aqs->aps/dot_general | solution.py:25
  293.0 25.1 %add_convert_fusion = bf16[4,896,896]{2,1,0:T(8,128)(2,1)} fusion(bf16[4,896,896]{2,1,0:T(8,128)(2,1)} %add_convert_fusion.1, bf16[4,896,896]{2,1,0:T(8,128)(2,1)} %convolution_convert_fusion.1), kind=kOutput, calls=%fused_computation.3 | convolution fusion | flops 11522015232 | bytes 19267584 | tf_op jit(solution)/shard_map/apq,aqs->aps/dot_general | solution.py:25
  318.1 10.5 %copy.30 = bf16[4,896,896]{2,0,1:T(4,128)(2,1)} copy(bf16[4,896,896]{2,1,0:T(8,128)(2,1)} %add_convert_fusion) | data formatting | bytes 12845056 | tf_op jit(solution)/shard_map/convert_element_type | solution.py:33
  328.6 5.3 all-to-all-start.3
  333.9 6.2 copy.24
  340.1 63.6 %all-to-all-done.3 = bf16[4,896,896]{2,0,1:T(4,128)(2,1)} async-done(((bf16[4,896,896]{2,0,1:T(4,128)(2,1)}), bf16[4,896,896]{2,0,1:T(4,128)(2,1)}, u32[]{:S(2)}, u32[]{:S(2)}) %all-to-all-start.3) | async-done | bytes 6422560 | tf_op jit(solution)/shard_map/all_to_all | solution.py:62
  403.6 5.5 all-to-all-start
  409.2 7.7 %copy.49 = bf16[4,4,224,896]{3,0,1,2:T(4,128)(2,1)} copy(bf16[4,4,224,896]{3,0,2,1:T(4,128)(2,1)} %bitcast.13) | data formatting | bytes 12845056 | tf_op jit(solution)/shard_map/all_to_all | solution.py:62
  416.9 11.0 %reshape.72 = bf16[16,224,896]{2,0,1:T(8,128)(2,1)} reshape(bf16[4,4,224,896]{3,1,0,2:T(4,128)(2,1)} %bitcast.68) | data formatting | bytes 12845056 | tf_op jit(solution)/shard_map/reshape.3
  427.9 7.4 %convolution_convert_fusion = bf16[16,224,896]{2,0,1:T(8,128)(2,1)} fusion(bf16[16,224,896]{2,0,1:T(8,128)(2,1)} %reshape.72, f32[16]{0:T(128)S(1)} %get-tuple-element.5, f32[16]{0:T(128)S(1)} %get-tuple-element.6), kind=kOutput, calls=%fused_computation.7 | convolution fusion | flops 105972736 | bytes 12845184 | tf_op jit(solution)/shard_map/tw,wkpq->tkpq/dot_general | solution.py:64
  435.3 11.5 %reshape.73 = bf16[4,4,1,4,56,896]{5,1,0,4,3,2:T(4,128)(2,1)} reshape(bf16[16,224,896]{2,0,1:T(8,128)(2,1)} %convolution_convert_fusion) | data formatting | bytes 12845056 | tf_op jit(solution)/shard_map/reshape | solution.py:68
  446.8 6.9 copy.32
  453.7 27.5 %all-to-all-done = bf16[4,2,4,2,56,896]{5,4,3,2,1,0:T(8,128)(2,1)} async-done(((bf16[4,2,4,2,56,896]{5,4,3,2,1,0:T(8,128)(2,1)}), bf16[4,2,4,2,56,896]{5,4,3,2,1,0:T(8,128)(2,1)}, u32[]{:S(2)}, u32[]{:S(2)}) %all-to-all-start) | async-done | bytes 6422560 | tf_op jit(solution)/shard_map/all_to_all | solution.py:51
  481.2 4.7 all-to-all-start.4
  485.9 0.0 all-reduce.3.cloned.1.call-start
  486.0 0.0 copy-done
  486.0 0.1 constant_dynamic-slice_fusion.1
  486.1 8.6 %bitcast_convert_fusion = f32[8,4,2,56,896]{4,3,2,1,0:T(8,128)} fusion(bf16[4,2,4,2,56,896]{5,4,3,2,1,0:T(8,128)(2,1)} %all-to-all-done), kind=kLoop, calls=%fused_computation.8 | loop fusion | flops 3211264 | bytes 19267584 | tf_op jit(solution)/shard_map/convert_element_type | solution.py:81
  494.7 133.2 %all-to-all-done.4 = bf16[16,4,1,56,896]{4,3,1,2,0:T(8,128)(2,1)} async-done(((bf16[16,4,1,56,896]{4,3,1,2,0:T(8,128)(2,1)}), bf16[16,4,1,56,896]{4,3,1,2,0:T(8,128)(2,1)}, u32[]{:S(2)}, u32[]{:S(2)}) %all-to-all-start.4) | async-done | bytes 6422560 | tf_op jit(solution)/shard_map/all_to_all | solution.py:71
  628.0 11.1 %copy.48 = bf16[4,2,2,4,1,56,896]{6,1,0,5,2,3,4:T(2,128)(2,1)} copy(bf16[4,2,2,4,1,56,896]{6,5,3,2,1,0,4:T(8,128)(2,1)} %bitcast.18) | data formatting | bytes 12845056 | tf_op jit(solution)/shard_map/reshape | solution.py:78
  639.0 13.9 %reshape.76 = bf16[8,4,2,56,896]{4,0,3,2,1:T(8,128)(2,1)} reshape(bf16[4,2,1,4,2,56,896]{6,1,0,5,4,3,2:T(2,128)(2,1)} %bitcast.69) | data formatting | bytes 12845056 | tf_op jit(solution)/shard_map/reshape | solution.py:79
  652.9 16.7 %fusion = bf16[8,4,2,56,896]{4,0,3,2,1:T(8,128)(2,1)} fusion(f32[8,4,2,56,896]{4,3,2,1,0:T(8,128)} %bitcast_convert_fusion, bf16[8,4,2,56,896]{4,0,3,2,1:T(8,128)(2,1)} %reshape.76, f32[8]{0:T(128)S(1)} %iota_multiply_fusion), kind=kOutput, calls=%fused_computation.2 | convolution fusion | flops 57803072 | bytes 25690144 | tf_op jit(solution)/shard_map/rk,ktlpq->rtlpq/dot_general | solution.py:80
  669.6 0.0 copy-start.2
  669.6 12.0 %multiply_reduce_fusion = f32[8,4,1024]{2,1,0:T(4,128)} fusion(f32[2,56,1024]{2,1,0:T(8,128)S(1)} %bitcast_convert_fusion.1, bf16[8,4,2,56,896]{4,0,3,2,1:T(8,128)(2,1)} %fusion, bf16[896,1024]{1,0:T(8,128)(2,1)S(1)} %copy-done), kind=kOutput, calls=%fused_computation | convolution fusion | flops 6583975936 | bytes 8847360 | tf_op jit(solution)/shard_map/rtlpq,qn->rtlpn/dot_general | solution.py:86
  681.6 0.0 all-reduce.3.cloned.1.call-update
  681.6 0.0 reduce-scatter.4.cloned.1.call-start
  681.7 0.0 copy-done.2
  681.7 0.6 dynamic-slice
  682.9 29.3 %all-reduce.3.cloned.1.call-done = f32[8,4,1024]{2,1,0:T(4,128)} async-done(((f32[8,4,1024]{2,1,0:T(4,128)}), f32[8,4,1024]{2,1,0:T(4,128)}) %all-reduce.3.cloned.1.call-update) | async-done | bytes 131088
  712.3 0.8 constant_dynamic-slice_fusion
  713.0 0.5 copy.39
  713.6 1.4 reshape.83
  715.0 0.0 reduce-scatter.4.cloned.1.call-update
  715.0 14.8 %reduce-scatter.4.cloned.1.call-done = f32[512,8]{1,0:T(8,128)} async-done(((f32[1024,8]{1,0:T(8,128)}), f32[512,8]{1,0:T(8,128)}) %reduce-scatter.4.cloned.1.call-update) | async-done | bytes 16400
  729.8 1.3 reshape.84
  731.0 0.8 copy.40
  (3 shorter events, 0.1 us)
Async XLA Ops:
  6.5 479.5 %copy-start = (bf16[896,1024]{1,0:T(8,128)(2,1)S(1)}, bf16[896,1024]{1,0:T(8,128)(2,1)}, u32[]{:S(2)}) copy-start(bf16[896,1024]{1,0:T(8,128)(2,1)} %param.5) | copy-start | bytes 5505028
  17.1 147.9 %all-to-all-start.1 = ((bf16[4,4,224,896]{3,1,2,0:T(4,128)(2,1)}), bf16[4,4,224,896]{3,1,2,0:T(4,128)(2,1)}, u32[]{:S(2)}, u32[]{:S(2)}) async-start(bf16[4,4,224,896]{3,1,2,0:T(4,128)(2,1)} %bitcast.66), calls=%async_computation.1 | async-start | bytes 12845056 | tf_op jit(solution)/shard_map/all_to_all | solution.py:56
  264.7 2.6 copy-start.1
  328.6 75.0 %all-to-all-start.3 = ((bf16[4,896,896]{2,0,1:T(4,128)(2,1)}), bf16[4,896,896]{2,0,1:T(4,128)(2,1)}, u32[]{:S(2)}, u32[]{:S(2)}) async-start(bf16[4,896,896]{2,0,1:T(4,128)(2,1)} %copy.30), calls=%async_computation.3 | async-start | bytes 12845056 | tf_op jit(solution)/shard_map/all_to_all | solution.py:62
  403.6 77.6 %all-to-all-start = ((bf16[4,2,4,2,56,896]{5,4,3,2,1,0:T(8,128)(2,1)}), bf16[4,2,4,2,56,896]{5,4,3,2,1,0:T(8,128)(2,1)}, u32[]{:S(2)}, u32[]{:S(2)}) async-start(bf16[4,2,4,2,56,896]{5,4,3,2,1,0:T(8,128)(2,1)} %copy.24), calls=%async_computation | async-start | bytes 12845056 | tf_op jit(solution)/shard_map/all_to_all | solution.py:51
  481.2 146.7 %all-to-all-start.4 = ((bf16[16,4,1,56,896]{4,3,1,2,0:T(8,128)(2,1)}), bf16[16,4,1,56,896]{4,3,1,2,0:T(8,128)(2,1)}, u32[]{:S(2)}, u32[]{:S(2)}) async-start(bf16[16,4,1,56,896]{4,3,1,2,0:T(8,128)(2,1)} %bitcast.65), calls=%async_computation.4 | async-start | bytes 12845056 | tf_op jit(solution)/shard_map/all_to_all | solution.py:71
  485.9 226.3 %all-reduce.3.cloned.1.call-start = ((), (), s32[]{:S(2)}) async-start(), calls=%async_computation.7 | async-start | bytes 262144
  669.6 12.1 %copy-start.2 = (u32[32]{0:T(128)S(1)}, u32[32]{0:T(128)}, u32[]{:S(2)}) copy-start(u32[32]{0:T(128)} %constant.44) | copy-start | bytes 388
  681.6 48.1 %reduce-scatter.4.cloned.1.call-start = ((), (), s32[]{:S(2)}) async-start(), calls=%async_computation.6 | async-start | bytes 786432
Sparse Core Ops, SparseCore 0:
  681.8 30.4 all-reduce.2
  715.1 14.6 reduce-scatter.3
